TPU v7x, 32 devices: a whole 2x2x4 slice. The times are simulated.
32 devices in a mesh: row: 4 (over y, core), col: 8 (over z, x).
Axes of the slice: x: 2, y: 2, z: 4, core: 2. Of those that a mesh axis runs over, the one named last changes fastest.
Arguments:
- residuals: bfloat16 [16384, 32], P(('row', 'col')), may hold values from -6 to 6
- intersect_blocks: int32 [32, 4], P(('row', 'col')), may hold values from 0 to 3
- local_inverse: bfloat16 [16384, 1024], P(('row', 'col')), may hold values from -0.1875 to 0.1875
- coarse_basis: float32 [32768, 64], P(('row', 'col')), may hold values from -0.1875 to 0.1875
- coarse_slots: int32 [2048], replicated, may hold values from 0 to 2047, each once
- coarse_inverse: float32 [2048, 2048], P('row', 'col'), may hold values from -0.5 to 0.5
Outputs:
- preconditioned: float32 [16384, 32], P(('row', 'col'))
Inputs may be any that keep to these rules, and one draw needn't show every extreme that they name: `intersect_blocks`: each entry names one of the four owned blocks. `coarse_slots`: every coarse index from 0 to 2047 appears exactly once.
All inputs are finite; a program needn't handle non-finite values.
Results may differ from a plain program's by a relative error of at most 0.0003.
Values may be sent and summed in bfloat16 or wider, within the bound.
A program may use at most 64 MiB of HBM per device.

v0:
```python
import jax
import jax.numpy as jnp
from jax import lax
from jax.sharding import PartitionSpec as P

BLK = 128


def extended(cells, sides, width, closed):
    for axis, dim in sides:
        count = lax.axis_size(axis)
        ends = count if closed else count - 1
        head = lax.slice_in_dim(cells, 0, width, axis=dim)
        tail = lax.slice_in_dim(cells, cells.shape[dim] - width, cells.shape[dim], axis=dim)
        cells = jnp.concatenate(
            [
                lax.ppermute(tail, axis, [(i, (i + 1) % count) for i in range(ends)]),
                cells,
                lax.ppermute(head, axis, [((i + 1) % count, i) for i in range(ends)]),
            ],
            axis=dim,
        )
    return cells


def shards(residuals, intersect_blocks, local_inverse, coarse_basis, coarse_slots, coarse_inverse):
    own_rows = residuals.shape[0]
    rhs_count = residuals.shape[1]
    nev_count = coarse_basis.shape[1]
    blocks = residuals.reshape(own_rows // BLK, BLK, rhs_count)
    send_index = intersect_blocks[0]
    outgoing = jnp.take(blocks, send_index, axis=0)
    padded = extended(outgoing[None, None], (("row", 0), ("col", 1)), 1, False)
    incoming = jnp.stack([padded[0, 1, 0], padded[2, 1, 1], padded[1, 0, 2], padded[1, 2, 3]])
    local_vec = jnp.concatenate([residuals, incoming.reshape(-1, rhs_count)], axis=0)
    schwarz = jnp.dot(local_inverse, local_vec, preferred_element_type=jnp.float32)
    partial_sums = jnp.dot(
        coarse_basis.T, local_vec.astype(jnp.float32), precision=lax.Precision.HIGHEST
    )
    column_width = coarse_inverse.shape[1]
    col_offset = lax.axis_index("col") * column_width

    def add_piece(carry, piece):
        shifted = lax.slice_in_dim(coarse_slots, 0, piece.shape[0], axis=0) - col_offset
        inside = (shifted >= 0) & (shifted < column_width)
        target = jnp.where(inside, shifted, column_width)
        return carry.at[target].add(piece, mode="drop")

    column_part = add_piece(
        jnp.zeros((column_width, rhs_count), jnp.float32),
        jax.tree.map(lambda a: lax.all_gather(a, ("row", "col"), axis=0, tiled=True), partial_sums),
    )
    product = jnp.dot(coarse_inverse, column_part, precision=lax.Precision.HIGHEST)
    row_total = lax.psum(product, "col")
    whole_coarse = lax.all_gather(row_total, "row", axis=0, tiled=True)
    my_slots = lax.dynamic_slice_in_dim(
        coarse_slots, lax.axis_index(("row", "col")) * nev_count, nev_count, 0
    )
    own_coarse = jnp.take(whole_coarse, my_slots, axis=0)
    prolonged = jnp.dot(coarse_basis, own_coarse, precision=lax.Precision.HIGHEST)
    returning = prolonged[own_rows:].reshape(-1, BLK, rhs_count)
    padded_back = extended(returning[None, None], (("row", 0), ("col", 1)), 1, False)
    returned = jnp.stack(
        [padded_back[2, 1, 0], padded_back[0, 1, 1], padded_back[1, 2, 2], padded_back[1, 0, 3]]
    )
    matches = (send_index[:, None] == jnp.arange(own_rows // BLK, dtype=jnp.int32)[None, :]).astype(
        jnp.float32
    )
    added = jnp.einsum("db,dkr->bkr", matches, returned, precision=lax.Precision.HIGHEST)
    return schwarz + prolonged[:own_rows] + added.reshape(own_rows, rhs_count)


def solution(mesh):
    placed = (
        P(("row", "col"), None),
        P(("row", "col"), None),
        P(("row", "col"), None),
        P(("row", "col"), None),
        P(),
        P("row", "col"),
    )
    return jax.shard_map(
        shards, mesh=mesh, in_specs=placed, out_specs=P(("row", "col"), None), check_vma=False
    )
```

profile of v0, /device:TPU:0, one launch (start us, length us, event | category | flops | bytes accessed | tf_op | source)
XLA Modules:
  0.0 212.3 jit_solution(17657866889500280651)
XLA Ops:
  6.5 0.8 fusion.18
  7.3 0.8 copy_bitcast_fusion
  8.1 0.6 gather_fusion
  8.8 2.4 %collective-permute-start = (bf16[1,1,4,128,32]{3,4,2,1,0:T(8,128)(2,1)S(1)}, bf16[1,1,4,128,32]{3,4,2,1,0:T(8,128)(2,1)S(1)}, u32[]{:S(2)}, u32[]{:S(2)}) collective-permute-start(bf16[1,1,4,128,32]{3,4,2,1,0:T(8,128)(2,1)S(1)} %bitcast_select_fusion), channel_id=1, source_target_pairs={{0,8},{8,16},{16,24},{1,9},{9,17},{17,25},{2,10},{10,18},{18,26},{... | collective-permute-start | bytes 98312 | tf_op jit(solution)/shard_map/ppermute | solution.py:17
  11.2 1.3 collective-permute-start.1
  12.6 3.8 %collective-permute-done.1 = bf16[1,1,4,128,32]{3,4,2,1,0:T(8,128)(2,1)S(1)} collective-permute-done((bf16[1,1,4,128,32]{3,4,2,1,0:T(8,128)(2,1)S(1)}, bf16[1,1,4,128,32]{3,4,2,1,0:T(8,128)(2,1)S(1)}, u32[]{:S(2)}, u32[]{:S(2)}) %collective-permute-start.1) | collective-permute-done | bytes 32800 | tf_op jit(solution)/shard_map/ppermute | solution.py:19
  16.4 1.3 collective-permute-start.3
  17.7 4.6 %collective-permute-start.2 = (bf16[3,1,4,128,32]{3,4,2,1,0:T(8,128)(2,1)S(1)}, bf16[3,1,4,128,32]{3,4,2,1,0:T(8,128)(2,1)S(1)}, u32[]{:S(2)}, u32[]{:S(2)}) collective-permute-start(bf16[3,1,4,128,32]{3,4,2,1,0:T(8,128)(2,1)S(1)} %pad_maximum_fusion), channel_id=1, source_target_pairs={{0,1},{1,2},{2,3},{3,4},{4,5},{5,6},{6,7},{8,9},{9,10},{10,11},{11... | collective-permute-start | bytes 294920 | tf_op jit(solution)/shard_map/ppermute | solution.py:17
  22.3 0.6 collective-permute-done.3
  22.9 3.2 %collective-permute-done.2 = bf16[3,1,4,128,32]{3,4,2,1,0:T(8,128)(2,1)S(1)} collective-permute-done((bf16[3,1,4,128,32]{3,4,2,1,0:T(8,128)(2,1)S(1)}, bf16[3,1,4,128,32]{3,4,2,1,0:T(8,128)(2,1)S(1)}, u32[]{:S(2)}, u32[]{:S(2)}) %collective-permute-start.2) | collective-permute-done | bytes 98336 | tf_op jit(solution)/shard_map/ppermute | solution.py:17
  26.4 68.6 %all-gather = f32[32,64,32]{1,2,0:T(8,128)S(1)} all-gather(f32[1,64,32]{1,2,0:T(8,128)S(1)} %convolution_bitcast_fusion.3), channel_id=1, replica_groups=mesh['row'=4,'col'=8] {'row','col'}, dimensions={0}, use_global_device_ids=true | all-gather | bytes 270336 | tf_op jit(solution)/shard_map/all_gather | solution.py:51
  95.4 11.5 %scatter_custom_fusion = f32[256,32]{1,0:T(8,128)S(1)} fusion(s32[2048]{0:T(1024)S(1)} %compare_select_fusion, f32[2048,32]{1,0:T(8,128)S(1)} %bitcast.68, f32[]{:T(128)} %constant.48.clone.1), kind=kCustom, calls=%fused_computation.18 | custom fusion | flops 65536 | bytes 32772 | tf_op jit(solution)/shard_map/scatter-add | solution.py:47
  106.9 1.3 convolution_bitcast_fusion.1
  108.2 68.8 %all-reduce.2.cloned.1.call-done = f32[512,32]{0,1:T(8,128)} async-done(((f32[512,32]{0,1:T(8,128)}), f32[512,32]{0,1:T(8,128)}) %all-reduce.2.cloned.1.call-update) | async-done | bytes 65552 | tf_op jit(solution)/shard_map/psum | solution.py:54
  177.0 6.0 %all_gather.7 = f32[2048,32]{0,1:T(8,128)S(1)} all-gather(f32[512,32]{0,1:T(8,128)} %all-reduce.2.cloned.1.call-done), channel_id=1, replica_groups=mesh['row'=4,'col'=8] {'row'}, dimensions={0}, use_global_device_ids=true | all-gather | bytes 327680 | tf_op jit(solution)/shard_map/all_gather | solution.py:55
  183.3 0.6 gather_fusion.1
  184.3 2.3 %collective-permute-start.5 = (f32[1,1,4,128,32]{3,4,2,1,0:T(8,128)S(1)}, f32[1,1,4,128,32]{3,4,2,1,0:T(8,128)S(1)}, u32[]{:S(2)}, u32[]{:S(2)}) collective-permute-start(f32[1,1,4,128,32]{3,4,2,1,0:T(8,128)S(1)} %copy.40), channel_id=1, source_target_pairs={{0,8},{8,16},{16,24},{1,9},{9,17},{17,25},{2,10},{10,18},{18,26},{... | collective-permute-start | bytes 196616 | tf_op jit(solution)/shard_map/ppermute | solution.py:17
  186.6 1.3 collective-permute-start.4
  187.9 2.5 %collective-permute-done.4 = f32[1,1,4,128,32]{3,4,2,1,0:T(8,128)S(1)} collective-permute-done((f32[1,1,4,128,32]{3,4,2,1,0:T(8,128)S(1)}, f32[1,1,4,128,32]{3,4,2,1,0:T(8,128)S(1)}, u32[]{:S(2)}, u32[]{:S(2)}) %collective-permute-start.4) | collective-permute-done | bytes 65568 | tf_op jit(solution)/shard_map/ppermute | solution.py:19
  190.5 1.3 collective-permute-start.6
  191.8 4.6 %collective-permute-start.7 = (f32[3,1,4,128,32]{3,4,2,1,0:T(8,128)S(1)}, f32[3,1,4,128,32]{3,4,2,1,0:T(8,128)S(1)}, u32[]{:S(2)}, u32[]{:S(2)}) collective-permute-start(f32[3,1,4,128,32]{3,4,2,1,0:T(8,128)S(1)} %constant_dynamic-update-slice_fusion.1), channel_id=1, source_target_pairs={{0,1},{1,2},{2,3},{3,4},{4,5},{5,6},{6,7},{8,9},{9,10},{10,11},{11... | collective-permute-start | bytes 589832 | tf_op jit(solution)/shard_map/ppermute | solution.py:17
  196.4 1.8 collective-permute-done.6
  198.2 6.0 %collective-permute-done.7 = f32[3,1,4,128,32]{3,4,2,1,0:T(8,128)S(1)} collective-permute-done((f32[3,1,4,128,32]{3,4,2,1,0:T(8,128)S(1)}, f32[3,1,4,128,32]{3,4,2,1,0:T(8,128)S(1)}, u32[]{:S(2)}, u32[]{:S(2)}) %collective-permute-start.7) | collective-permute-done | bytes 196640 | tf_op jit(solution)/shard_map/ppermute | solution.py:17
  204.4 1.1 fusion.1
  (50 shorter events, 1.9 us)
Async XLA Ops:
  6.5 197.9 %copy-start = (bf16[512,1024]{1,0:T(8,128)(2,1)S(1)}, bf16[512,1024]{1,0:T(8,128)(2,1)}, u32[]{:S(2)}) copy-start(bf16[512,1024]{1,0:T(8,128)(2,1)} %param.8) | copy-start | bytes 3145732
  6.5 0.8 copy-start.7
  6.5 170.4 %all-reduce.2.cloned.1.call-start = ((), (), s32[]{:S(2)}) async-start(), calls=%async_computation | async-start | bytes 131072 | tf_op jit(solution)/shard_map/psum | solution.py:54
  8.1 4.4 %copy-start.3 = (bf16[512,32]{0,1:T(8,128)(2,1)S(1)}, bf16[512,32]{0,1:T(8,128)(2,1)}, u32[]{:S(2)}) copy-start(bf16[512,32]{0,1:T(8,128)(2,1)} %param.6) | copy-start | bytes 98308
  8.1 4.4 %copy-start.6 = (s32[2048]{0:T(1024)S(1)}, s32[2048]{0:T(1024)}, u32[]{:S(2)}) copy-start(s32[2048]{0:T(1024)} %param.10) | copy-start | bytes 24580
  8.7 17.5 %copy-start.1 = (f32[1024,64]{0,1:T(8,128)S(1)}, f32[1024,64]{0,1:T(8,128)}, u32[]{:S(2)}) copy-start(f32[1024,64]{0,1:T(8,128)} %param.9) | copy-start | bytes 786436
  8.8 3.8 %collective-permute-start = (bf16[1,1,4,128,32]{3,4,2,1,0:T(8,128)(2,1)S(1)}, bf16[1,1,4,128,32]{3,4,2,1,0:T(8,128)(2,1)S(1)}, u32[]{:S(2)}, u32[]{:S(2)}) collective-permute-start(bf16[1,1,4,128,32]{3,4,2,1,0:T(8,128)(2,1)S(1)} %bitcast_select_fusion), channel_id=1, source_target_pairs={{0,8},{8,16},{16,24},{1,9},{9,17},{17,25},{2,10},{10,18},{18,26},{... | collective-permute-start | bytes 98312 | tf_op jit(solution)/shard_map/ppermute | solution.py:17
  11.2 5.2 %collective-permute-start.1 = (bf16[1,1,4,128,32]{3,4,2,1,0:T(8,128)(2,1)S(1)}, bf16[1,1,4,128,32]{3,4,2,1,0:T(8,128)(2,1)S(1)}, u32[]{:S(2)}, u32[]{:S(2)}) collective-permute-start(bf16[1,1,4,128,32]{3,4,2,1,0:T(8,128)(2,1)S(1)} %bitcast_select_fusion), channel_id=1, source_target_pairs={{8,0},{16,8},{24,16},{9,1},{17,9},{25,17},{10,2},{18,10},{26,18},{... | collective-permute-start | bytes 98312 | tf_op jit(solution)/shard_map/ppermute | solution.py:19
  16.4 6.5 %collective-permute-start.3 = (bf16[3,1,4,128,32]{3,4,2,1,0:T(8,128)(2,1)S(1)}, bf16[3,1,4,128,32]{3,4,2,1,0:T(8,128)(2,1)S(1)}, u32[]{:S(2)}, u32[]{:S(2)}) collective-permute-start(bf16[3,1,4,128,32]{3,4,2,1,0:T(8,128)(2,1)S(1)} %pad_maximum_fusion), channel_id=1, source_target_pairs={{1,0},{2,1},{3,2},{4,3},{5,4},{6,5},{7,6},{9,8},{10,9},{11,10},{12... | collective-permute-start | bytes 294920 | tf_op jit(solution)/shard_map/ppermute | solution.py:19
  17.7 8.4 %collective-permute-start.2 = (bf16[3,1,4,128,32]{3,4,2,1,0:T(8,128)(2,1)S(1)}, bf16[3,1,4,128,32]{3,4,2,1,0:T(8,128)(2,1)S(1)}, u32[]{:S(2)}, u32[]{:S(2)}) collective-permute-start(bf16[3,1,4,128,32]{3,4,2,1,0:T(8,128)(2,1)S(1)} %pad_maximum_fusion), channel_id=1, source_target_pairs={{0,1},{1,2},{2,3},{3,4},{4,5},{5,6},{6,7},{8,9},{9,10},{10,11},{11... | collective-permute-start | bytes 294920 | tf_op jit(solution)/shard_map/ppermute | solution.py:17
  95.0 11.9 %copy-start.2 = (f32[512,256]{1,0:T(8,128)S(1)}, f32[512,256]{1,0:T(8,128)}, u32[]{:S(2)}) copy-start(f32[512,256]{1,0:T(8,128)} %param.11) | copy-start | bytes 1572868
  184.3 3.6 %collective-permute-start.5 = (f32[1,1,4,128,32]{3,4,2,1,0:T(8,128)S(1)}, f32[1,1,4,128,32]{3,4,2,1,0:T(8,128)S(1)}, u32[]{:S(2)}, u32[]{:S(2)}) collective-permute-start(f32[1,1,4,128,32]{3,4,2,1,0:T(8,128)S(1)} %copy.40), channel_id=1, source_target_pairs={{0,8},{8,16},{16,24},{1,9},{9,17},{17,25},{2,10},{10,18},{18,26},{... | collective-permute-start | bytes 196616 | tf_op jit(solution)/shard_map/ppermute | solution.py:17
  186.6 3.9 %collective-permute-start.4 = (f32[1,1,4,128,32]{3,4,2,1,0:T(8,128)S(1)}, f32[1,1,4,128,32]{3,4,2,1,0:T(8,128)S(1)}, u32[]{:S(2)}, u32[]{:S(2)}) collective-permute-start(f32[1,1,4,128,32]{3,4,2,1,0:T(8,128)S(1)} %copy.40), channel_id=1, source_target_pairs={{8,0},{16,8},{24,16},{9,1},{17,9},{25,17},{10,2},{18,10},{26,18},{... | collective-permute-start | bytes 196616 | tf_op jit(solution)/shard_map/ppermute | solution.py:19
  187.9 8.5 %copy-start.4 = (f32[1,1,4,128,32]{3,4,2,1,0:T(8,128)}, f32[1,1,4,128,32]{3,4,2,1,0:T(8,128)S(1)}, u32[]{:S(2)}) copy-start(f32[1,1,4,128,32]{3,4,2,1,0:T(8,128)S(1)} %collective-permute-done.5) | copy-start | bytes 196612
  190.5 5.9 %copy-start.5 = (f32[1,1,4,128,32]{3,4,2,1,0:T(8,128)}, f32[1,1,4,128,32]{3,4,2,1,0:T(8,128)S(1)}, u32[]{:S(2)}) copy-start(f32[1,1,4,128,32]{3,4,2,1,0:T(8,128)S(1)} %collective-permute-done.4) | copy-start | bytes 196612
  190.5 7.7 %collective-permute-start.6 = (f32[3,1,4,128,32]{3,4,2,1,0:T(8,128)S(1)}, f32[3,1,4,128,32]{3,4,2,1,0:T(8,128)S(1)}, u32[]{:S(2)}, u32[]{:S(2)}) collective-permute-start(f32[3,1,4,128,32]{3,4,2,1,0:T(8,128)S(1)} %constant_dynamic-update-slice_fusion.1), channel_id=1, source_target_pairs={{1,0},{2,1},{3,2},{4,3},{5,4},{6,5},{7,6},{9,8},{10,9},{11,10},{12... | collective-permute-start | bytes 589832 | tf_op jit(solution)/shard_map/ppermute | solution.py:19
  191.8 12.4 %collective-permute-start.7 = (f32[3,1,4,128,32]{3,4,2,1,0:T(8,128)S(1)}, f32[3,1,4,128,32]{3,4,2,1,0:T(8,128)S(1)}, u32[]{:S(2)}, u32[]{:S(2)}) collective-permute-start(f32[3,1,4,128,32]{3,4,2,1,0:T(8,128)S(1)} %constant_dynamic-update-slice_fusion.1), channel_id=1, source_target_pairs={{0,1},{1,2},{2,3},{3,4},{4,5},{5,6},{6,7},{8,9},{9,10},{10,11},{11... | collective-permute-start | bytes 589832 | tf_op jit(solution)/shard_map/ppermute | solution.py:17
  198.2 6.0 %slice-start = ((f32[1,1,4,128,32]{3,4,2,1,0:T(8,128)}), f32[1,1,1,128,32]{3,4,2,1,0:T(8,128)S(1)}, s32[]{:S(2)}) async-start(f32[1,1,4,128,32]{3,4,2,1,0:T(8,128)} %copy-done.4), calls=%async_computation.1 | async-start | bytes 32768 | tf_op jit(solution)/shard_map/slice | solution.py:64
  198.2 6.0 %slice-start.1 = ((f32[1,1,4,128,32]{3,4,2,1,0:T(8,128)}), f32[1,1,1,128,32]{3,4,2,1,0:T(8,128)S(1)}, s32[]{:S(2)}) async-start(f32[1,1,4,128,32]{3,4,2,1,0:T(8,128)} %copy-done.5), calls=%async_computation.2 | async-start | bytes 32768 | tf_op jit(solution)/shard_map/slice | solution.py:64
Sparse Core Ops, SparseCore 0:
  108.3 68.6 all-reduce.1
where the time goes:
time: 213 us; the launch traced here: 212 us
  waiting for transfers between devices  86.8 us (41%)
  blocking collectives  74.5 us (35%)
  starting transfers between devices  18.9 us (9%)
  between operations  13.7 us (6%)
  other arithmetic  12.5 us (6%)
  matrix products  3.19 us (1%)
  local copies, waits for them, and re-layouts  2.73 us (1%)
    psum x1, waiting for transfers between devices, shards(): row_total = lax.psum(product, 'col')  68.8 us
    all_gather x1, blocking collectives, shards(): lax.all_gather(a, ('row', 'col'), axis=0, tiled=True)  68.6 us
    ppermute x4, starting transfers between devices, extended(): lax.ppermute(tail, axis, [(i, (i + 1) % count) for i in range(ends)])  13.8 us
    scatter-add x1, other arithmetic, add_piece(): return carry.at[target].add(piece, mode='drop')  11.5 us
    ppermute x4, waiting for transfers between devices, extended(): lax.ppermute(tail, axis, [(i, (i + 1) % count) for i in range(ends)])  9.19 us
    ppermute x4, waiting for transfers between devices, extended(): lax.ppermute(head, axis, [((i + 1) % count, i) for i in range(ends)])  8.76 us
    all_gather x1, blocking collectives, shards(): whole_coarse = lax.all_gather(row_total, 'row', axis=0, tiled=True)  5.97 us
    ppermute x4, starting transfers between devices, extended(): lax.ppermute(head, axis, [((i + 1) % count, i) for i in range(ends)])  5.17 us
  transfers between devices with their start and end apart: 9, of which 7 were waited for; matrix products, arithmetic and copies ran while one was open for 0% of the time, Pallas kernels for 0%

commit v1 on v0

--- a/solution.py
+++ b/solution.py
@@ -4,6 +4,20 @@
 from jax.sharding import PartitionSpec as P
 
 BLK = 128
+
+
+def list_marks(mine_x):
+    n_slots = lax.axis_size("col")
+    z2 = mine_x
+    for to_i in [j for j in (1, 2, 4, 8, 16) if j < n_slots]:
+        kept_rows = []
+        ii = 0
+        while ii < n_slots:
+            kept_rows.append((ii, ii ^ to_i))
+            ii = ii + 1
+        piece_now = lax.ppermute(z2, "col", kept_rows)
+        z2 = z2 + piece_now
+    return z2
 
 
 def extended(cells, sides, width, closed):
@@ -51,7 +65,7 @@
         jax.tree.map(lambda a: lax.all_gather(a, ("row", "col"), axis=0, tiled=True), partial_sums),
     )
     product = jnp.dot(coarse_inverse, column_part, precision=lax.Precision.HIGHEST)
-    row_total = lax.psum(product, "col")
+    row_total = list_marks(product)
     whole_coarse = lax.all_gather(row_total, "row", axis=0, tiled=True)
     my_slots = lax.dynamic_slice_in_dim(
         coarse_slots, lax.axis_index(("row", "col")) * nev_count, nev_count, 0

time: 213 us -> 144 us (0.68)
  waiting for transfers between devices: 86.8 us -> 29.9 us
  between operations: 13.7 us -> 0.36 us
    psum x1 -> x0, waiting for transfers between devices: 68.8 us -> none  [shards(): row_total = lax.psum(product, 'col')]
    ppermute x0 -> x3, waiting for transfers between devices: none -> 13.7 us  [list_marks(): piece_now = lax.ppermute(z2, 'col', kept_rows)]
  transfers between devices with their start and end apart: 9 -> 11, of which waited for: 7 -> 9; matrix products, arithmetic and copies ran while one was open for 0% -> 0% of each run, Pallas kernels for 0% -> 0%
where the time goes in v1:
time: 144 us
  blocking collectives  76.4 us (53%)
  waiting for transfers between devices  29.9 us (21%)
  starting transfers between devices  19.1 us (13%)
  other arithmetic  12.5 us (9%)
  local copies, waits for them, and re-layouts  2.73 us (2%)
  matrix products  2.55 us (2%)
    all_gather x1, blocking collectives, shards(): lax.all_gather(a, ('row', 'col'), axis=0, tiled=True)  68.6 us
    ppermute x4, starting transfers between devices, extended(): lax.ppermute(tail, axis, [(i, (i + 1) % count) for i in range(ends)])  13.8 us
    ppermute x3, waiting for transfers between devices, list_marks(): piece_now = lax.ppermute(z2, 'col', kept_rows)  13.7 us
    scatter-add x1, other arithmetic, add_piece(): return carry.at[target].add(piece, mode='drop')  11.5 us
    ppermute x4, waiting for transfers between devices, extended(): lax.ppermute(head, axis, [((i + 1) % count, i) for i in range(ends)])  8.9 us
    all_gather x1, blocking collectives, shards(): whole_coarse = lax.all_gather(row_total, 'row', axis=0, tiled=True)  7.88 us
    ppermute x4, waiting for transfers between devices, extended(): lax.ppermute(tail, axis, [(i, (i + 1) % count) for i in range(ends)])  7.33 us
    ppermute x4, starting transfers between devices, extended(): lax.ppermute(head, axis, [((i + 1) % count, i) for i in range(ends)])  5.17 us
  transfers between devices with their start and end apart: 11, of which 9 were waited for; matrix products, arithmetic and copies ran while one was open for 0% of the time, Pallas kernels for 0%

profile of v1, /device:TPU:0, one launch (start us, length us, event | category | flops | bytes accessed | tf_op | source)
XLA Modules:
  0.0 143.6 jit_solution(4675946628942659227)
XLA Ops:
  0.0 0.8 fusion.18
  0.8 0.8 copy_bitcast_fusion
  2.2 2.4 %collective-permute-start = (bf16[1,1,4,128,32]{3,4,2,1,0:T(8,128)(2,1)S(1)}, bf16[1,1,4,128,32]{3,4,2,1,0:T(8,128)(2,1)S(1)}, u32[]{:S(2)}, u32[]{:S(2)}) collective-permute-start(bf16[1,1,4,128,32]{3,4,2,1,0:T(8,128)(2,1)S(1)} %bitcast_select_fusion), channel_id=1, source_target_pairs={{0,8},{8,16},{16,24},{1,9},{9,17},{17,25},{2,10},{10,18},{18,26},{... | collective-permute-start | bytes 98312 | tf_op jit(solution)/shard_map/ppermute | solution.py:31
  4.6 1.3 collective-permute-start.1
  6.0 3.9 %collective-permute-done.1 = bf16[1,1,4,128,32]{3,4,2,1,0:T(8,128)(2,1)S(1)} collective-permute-done((bf16[1,1,4,128,32]{3,4,2,1,0:T(8,128)(2,1)S(1)}, bf16[1,1,4,128,32]{3,4,2,1,0:T(8,128)(2,1)S(1)}, u32[]{:S(2)}, u32[]{:S(2)}) %collective-permute-start.1) | collective-permute-done | bytes 32800 | tf_op jit(solution)/shard_map/ppermute | solution.py:33
  9.9 1.3 collective-permute-start.3
  11.2 4.6 %collective-permute-start.2 = (bf16[3,1,4,128,32]{3,4,2,1,0:T(8,128)(2,1)S(1)}, bf16[3,1,4,128,32]{3,4,2,1,0:T(8,128)(2,1)S(1)}, u32[]{:S(2)}, u32[]{:S(2)}) collective-permute-start(bf16[3,1,4,128,32]{3,4,2,1,0:T(8,128)(2,1)S(1)} %pad_maximum_fusion), channel_id=1, source_target_pairs={{0,1},{1,2},{2,3},{3,4},{4,5},{5,6},{6,7},{8,9},{9,10},{10,11},{11... | collective-permute-start | bytes 294920 | tf_op jit(solution)/shard_map/ppermute | solution.py:31
  15.7 0.6 collective-permute-done.3
  16.4 3.2 %collective-permute-done.2 = bf16[3,1,4,128,32]{3,4,2,1,0:T(8,128)(2,1)S(1)} collective-permute-done((bf16[3,1,4,128,32]{3,4,2,1,0:T(8,128)(2,1)S(1)}, bf16[3,1,4,128,32]{3,4,2,1,0:T(8,128)(2,1)S(1)}, u32[]{:S(2)}, u32[]{:S(2)}) %collective-permute-start.2) | collective-permute-done | bytes 98336 | tf_op jit(solution)/shard_map/ppermute | solution.py:31
  19.9 68.6 %all-gather = f32[32,64,32]{1,2,0:T(8,128)S(1)} all-gather(f32[1,64,32]{1,2,0:T(8,128)S(1)} %convolution_bitcast_fusion.3), channel_id=1, replica_groups=mesh['row'=4,'col'=8] {'row','col'}, dimensions={0}, use_global_device_ids=true | all-gather | bytes 270336 | tf_op jit(solution)/shard_map/all_gather | solution.py:65
  88.8 11.5 %scatter_custom_fusion = f32[256,32]{1,0:T(8,128)S(1)} fusion(s32[2048]{0:T(1024)S(1)} %compare_select_fusion, f32[2048,32]{1,0:T(8,128)S(1)} %bitcast.68, f32[]{:T(128)} %constant.48.clone.1), kind=kCustom, calls=%fused_computation.18 | custom fusion | flops 65536 | bytes 32772 | tf_op jit(solution)/shard_map/scatter-add | solution.py:61
  100.3 0.6 convolution_bitcast_fusion.1
  101.0 4.2 %collective-permute-done.4 = f32[512,32]{0,1:T(8,128)S(1)} collective-permute-done((f32[512,32]{0,1:T(8,128)S(1)}, f32[512,32]{0,1:T(8,128)S(1)}, u32[]{:S(2)}, u32[]{:S(2)}) %collective-permute-start.4) | collective-permute-done | bytes 65568 | tf_op jit(solution)/shard_map/ppermute | solution.py:18
  105.5 4.2 %collective-permute-done.5 = f32[512,32]{0,1:T(8,128)S(1)} collective-permute-done((f32[512,32]{0,1:T(8,128)S(1)}, f32[512,32]{0,1:T(8,128)S(1)}, u32[]{:S(2)}, u32[]{:S(2)}) %collective-permute-start.5) | collective-permute-done | bytes 65568 | tf_op jit(solution)/shard_map/ppermute | solution.py:18
  109.7 5.3 %collective-permute-done.6 = f32[512,32]{0,1:T(8,128)S(1)} collective-permute-done((f32[512,32]{0,1:T(8,128)S(1)}, f32[512,32]{0,1:T(8,128)S(1)}, u32[]{:S(2)}, u32[]{:S(2)}) %collective-permute-start.6) | collective-permute-done | bytes 65568 | tf_op jit(solution)/shard_map/ppermute | solution.py:18
  115.0 7.9 %all_gather.7 = f32[2048,32]{0,1:T(8,128)S(1)} all-gather(f32[512,32]{0,1:T(8,128)S(1)} %add.58), channel_id=1, replica_groups=mesh['row'=4,'col'=8] {'row'}, dimensions={0}, use_global_device_ids=true | all-gather | bytes 327680 | tf_op jit(solution)/shard_map/all_gather | solution.py:69
  124.3 2.3 %collective-permute-start.8 = (f32[1,1,4,128,32]{3,4,2,1,0:T(8,128)S(1)}, f32[1,1,4,128,32]{3,4,2,1,0:T(8,128)S(1)}, u32[]{:S(2)}, u32[]{:S(2)}) collective-permute-start(f32[1,1,4,128,32]{3,4,2,1,0:T(8,128)S(1)} %copy.42), channel_id=1, source_target_pairs={{0,8},{8,16},{16,24},{1,9},{9,17},{17,25},{2,10},{10,18},{18,26},{... | collective-permute-start | bytes 196616 | tf_op jit(solution)/shard_map/ppermute | solution.py:31
  126.6 1.3 collective-permute-start.7
  127.9 2.6 %collective-permute-done.7 = f32[1,1,4,128,32]{3,4,2,1,0:T(8,128)S(1)} collective-permute-done((f32[1,1,4,128,32]{3,4,2,1,0:T(8,128)S(1)}, f32[1,1,4,128,32]{3,4,2,1,0:T(8,128)S(1)}, u32[]{:S(2)}, u32[]{:S(2)}) %collective-permute-start.7) | collective-permute-done | bytes 65568 | tf_op jit(solution)/shard_map/ppermute | solution.py:33
  130.5 1.3 collective-permute-start.9
  131.8 4.6 %collective-permute-start.10 = (f32[3,1,4,128,32]{3,4,2,1,0:T(8,128)S(1)}, f32[3,1,4,128,32]{3,4,2,1,0:T(8,128)S(1)}, u32[]{:S(2)}, u32[]{:S(2)}) collective-permute-start(f32[3,1,4,128,32]{3,4,2,1,0:T(8,128)S(1)} %constant_dynamic-update-slice_fusion.1), channel_id=1, source_target_pairs={{0,1},{1,2},{2,3},{3,4},{4,5},{5,6},{6,7},{8,9},{9,10},{10,11},{11... | collective-permute-start | bytes 589832 | tf_op jit(solution)/shard_map/ppermute | solution.py:31
  136.4 1.8 %collective-permute-done.9 = f32[3,1,4,128,32]{3,4,2,1,0:T(8,128)S(1)} collective-permute-done((f32[3,1,4,128,32]{3,4,2,1,0:T(8,128)S(1)}, f32[3,1,4,128,32]{3,4,2,1,0:T(8,128)S(1)}, u32[]{:S(2)}, u32[]{:S(2)}) %collective-permute-start.9) | collective-permute-done | bytes 196640 | tf_op jit(solution)/shard_map/ppermute | solution.py:33
  138.2 4.1 %collective-permute-done.10 = f32[3,1,4,128,32]{3,4,2,1,0:T(8,128)S(1)} collective-permute-done((f32[3,1,4,128,32]{3,4,2,1,0:T(8,128)S(1)}, f32[3,1,4,128,32]{3,4,2,1,0:T(8,128)S(1)}, u32[]{:S(2)}, u32[]{:S(2)}) %collective-permute-start.10) | collective-permute-done | bytes 196640 | tf_op jit(solution)/shard_map/ppermute | solution.py:31
  142.6 1.1 fusion.1
  (56 shorter events, 3.3 us)
Async XLA Ops:
  0.0 142.6 %copy-start = (bf16[512,1024]{1,0:T(8,128)(2,1)S(1)}, bf16[512,1024]{1,0:T(8,128)(2,1)}, u32[]{:S(2)}) copy-start(bf16[512,1024]{1,0:T(8,128)(2,1)} %param.8) | copy-start | bytes 3145732
  0.0 0.8 copy-start.7
  1.6 4.4 %copy-start.6 = (s32[2048]{0:T(1024)S(1)}, s32[2048]{0:T(1024)}, u32[]{:S(2)}) copy-start(s32[2048]{0:T(1024)} %param.10) | copy-start | bytes 24580
  1.6 4.4 %copy-start.3 = (bf16[512,32]{0,1:T(8,128)(2,1)S(1)}, bf16[512,32]{0,1:T(8,128)(2,1)}, u32[]{:S(2)}) copy-start(bf16[512,32]{0,1:T(8,128)(2,1)} %param.6) | copy-start | bytes 98308
  2.1 17.5 %copy-start.1 = (f32[1024,64]{0,1:T(8,128)S(1)}, f32[1024,64]{0,1:T(8,128)}, u32[]{:S(2)}) copy-start(f32[1024,64]{0,1:T(8,128)} %param.9) | copy-start | bytes 786436
  2.2 3.8 %collective-permute-start = (bf16[1,1,4,128,32]{3,4,2,1,0:T(8,128)(2,1)S(1)}, bf16[1,1,4,128,32]{3,4,2,1,0:T(8,128)(2,1)S(1)}, u32[]{:S(2)}, u32[]{:S(2)}) collective-permute-start(bf16[1,1,4,128,32]{3,4,2,1,0:T(8,128)(2,1)S(1)} %bitcast_select_fusion), channel_id=1, source_target_pairs={{0,8},{8,16},{16,24},{1,9},{9,17},{17,25},{2,10},{10,18},{18,26},{... | collective-permute-start | bytes 98312 | tf_op jit(solution)/shard_map/ppermute | solution.py:31
  4.6 5.2 %collective-permute-start.1 = (bf16[1,1,4,128,32]{3,4,2,1,0:T(8,128)(2,1)S(1)}, bf16[1,1,4,128,32]{3,4,2,1,0:T(8,128)(2,1)S(1)}, u32[]{:S(2)}, u32[]{:S(2)}) collective-permute-start(bf16[1,1,4,128,32]{3,4,2,1,0:T(8,128)(2,1)S(1)} %bitcast_select_fusion), channel_id=1, source_target_pairs={{8,0},{16,8},{24,16},{9,1},{17,9},{25,17},{10,2},{18,10},{26,18},{... | collective-permute-start | bytes 98312 | tf_op jit(solution)/shard_map/ppermute | solution.py:33
  9.9 6.5 %collective-permute-start.3 = (bf16[3,1,4,128,32]{3,4,2,1,0:T(8,128)(2,1)S(1)}, bf16[3,1,4,128,32]{3,4,2,1,0:T(8,128)(2,1)S(1)}, u32[]{:S(2)}, u32[]{:S(2)}) collective-permute-start(bf16[3,1,4,128,32]{3,4,2,1,0:T(8,128)(2,1)S(1)} %pad_maximum_fusion), channel_id=1, source_target_pairs={{1,0},{2,1},{3,2},{4,3},{5,4},{6,5},{7,6},{9,8},{10,9},{11,10},{12... | collective-permute-start | bytes 294920 | tf_op jit(solution)/shard_map/ppermute | solution.py:33
  11.2 8.4 %collective-permute-start.2 = (bf16[3,1,4,128,32]{3,4,2,1,0:T(8,128)(2,1)S(1)}, bf16[3,1,4,128,32]{3,4,2,1,0:T(8,128)(2,1)S(1)}, u32[]{:S(2)}, u32[]{:S(2)}) collective-permute-start(bf16[3,1,4,128,32]{3,4,2,1,0:T(8,128)(2,1)S(1)} %pad_maximum_fusion), channel_id=1, source_target_pairs={{0,1},{1,2},{2,3},{3,4},{4,5},{5,6},{6,7},{8,9},{9,10},{10,11},{11... | collective-permute-start | bytes 294920 | tf_op jit(solution)/shard_map/ppermute | solution.py:31
  88.5 11.9 %copy-start.2 = (f32[512,256]{1,0:T(8,128)S(1)}, f32[512,256]{1,0:T(8,128)}, u32[]{:S(2)}) copy-start(f32[512,256]{1,0:T(8,128)} %param.11) | copy-start | bytes 1572868
  101.0 4.3 %collective-permute-start.4 = (f32[512,32]{0,1:T(8,128)S(1)}, f32[512,32]{0,1:T(8,128)S(1)}, u32[]{:S(2)}, u32[]{:S(2)}) collective-permute-start(f32[512,32]{0,1:T(8,128)S(1)} %convolution_bitcast_fusion.1), channel_id=1, source_target_pairs={{0,1},{1,0},{2,3},{3,2},{4,5},{5,4},{6,7},{7,6},{8,9},{9,8},{10,11... | collective-permute-start | bytes 196616 | tf_op jit(solution)/shard_map/ppermute | solution.py:18
  105.3 4.3 %collective-permute-start.5 = (f32[512,32]{0,1:T(8,128)S(1)}, f32[512,32]{0,1:T(8,128)S(1)}, u32[]{:S(2)}, u32[]{:S(2)}) collective-permute-start(f32[512,32]{0,1:T(8,128)S(1)} %add.56), channel_id=1, source_target_pairs={{0,2},{1,3},{2,0},{3,1},{4,6},{5,7},{6,4},{7,5},{8,10},{9,11},{10,... | collective-permute-start | bytes 196616 | tf_op jit(solution)/shard_map/ppermute | solution.py:18
  109.6 5.4 %collective-permute-start.6 = (f32[512,32]{0,1:T(8,128)S(1)}, f32[512,32]{0,1:T(8,128)S(1)}, u32[]{:S(2)}, u32[]{:S(2)}) collective-permute-start(f32[512,32]{0,1:T(8,128)S(1)} %add.57), channel_id=1, source_target_pairs={{0,4},{1,5},{2,6},{3,7},{4,0},{5,1},{6,2},{7,3},{8,12},{9,13},{10,... | collective-permute-start | bytes 196616 | tf_op jit(solution)/shard_map/ppermute | solution.py:18
  124.3 3.6 %collective-permute-start.8 = (f32[1,1,4,128,32]{3,4,2,1,0:T(8,128)S(1)}, f32[1,1,4,128,32]{3,4,2,1,0:T(8,128)S(1)}, u32[]{:S(2)}, u32[]{:S(2)}) collective-permute-start(f32[1,1,4,128,32]{3,4,2,1,0:T(8,128)S(1)} %copy.42), channel_id=1, source_target_pairs={{0,8},{8,16},{16,24},{1,9},{9,17},{17,25},{2,10},{10,18},{18,26},{... | collective-permute-start | bytes 196616 | tf_op jit(solution)/shard_map/ppermute | solution.py:31
  126.6 3.9 %collective-permute-start.7 = (f32[1,1,4,128,32]{3,4,2,1,0:T(8,128)S(1)}, f32[1,1,4,128,32]{3,4,2,1,0:T(8,128)S(1)}, u32[]{:S(2)}, u32[]{:S(2)}) collective-permute-start(f32[1,1,4,128,32]{3,4,2,1,0:T(8,128)S(1)} %copy.42), channel_id=1, source_target_pairs={{8,0},{16,8},{24,16},{9,1},{17,9},{25,17},{10,2},{18,10},{26,18},{... | collective-permute-start | bytes 196616 | tf_op jit(solution)/shard_map/ppermute | solution.py:33
  127.9 8.5 %copy-start.4 = (f32[1,1,4,128,32]{3,4,2,1,0:T(8,128)}, f32[1,1,4,128,32]{3,4,2,1,0:T(8,128)S(1)}, u32[]{:S(2)}) copy-start(f32[1,1,4,128,32]{3,4,2,1,0:T(8,128)S(1)} %collective-permute-done.8) | copy-start | bytes 196612
  130.5 5.9 %copy-start.5 = (f32[1,1,4,128,32]{3,4,2,1,0:T(8,128)}, f32[1,1,4,128,32]{3,4,2,1,0:T(8,128)S(1)}, u32[]{:S(2)}) copy-start(f32[1,1,4,128,32]{3,4,2,1,0:T(8,128)S(1)} %collective-permute-done.7) | copy-start | bytes 196612
  130.5 7.7 %collective-permute-start.9 = (f32[3,1,4,128,32]{3,4,2,1,0:T(8,128)S(1)}, f32[3,1,4,128,32]{3,4,2,1,0:T(8,128)S(1)}, u32[]{:S(2)}, u32[]{:S(2)}) collective-permute-start(f32[3,1,4,128,32]{3,4,2,1,0:T(8,128)S(1)} %constant_dynamic-update-slice_fusion.1), channel_id=1, source_target_pairs={{1,0},{2,1},{3,2},{4,3},{5,4},{6,5},{7,6},{9,8},{10,9},{11,10},{12... | collective-permute-start | bytes 589832 | tf_op jit(solution)/shard_map/ppermute | solution.py:33
  131.8 10.5 %collective-permute-start.10 = (f32[3,1,4,128,32]{3,4,2,1,0:T(8,128)S(1)}, f32[3,1,4,128,32]{3,4,2,1,0:T(8,128)S(1)}, u32[]{:S(2)}, u32[]{:S(2)}) collective-permute-start(f32[3,1,4,128,32]{3,4,2,1,0:T(8,128)S(1)} %constant_dynamic-update-slice_fusion.1), channel_id=1, source_target_pairs={{0,1},{1,2},{2,3},{3,4},{4,5},{5,6},{6,7},{8,9},{9,10},{10,11},{11... | collective-permute-start | bytes 589832 | tf_op jit(solution)/shard_map/ppermute | solution.py:31
  138.2 4.1 %slice-start = ((f32[1,1,4,128,32]{3,4,2,1,0:T(8,128)}), f32[1,1,1,128,32]{3,4,2,1,0:T(8,128)S(1)}, s32[]{:S(2)}) async-start(f32[1,1,4,128,32]{3,4,2,1,0:T(8,128)} %copy-done.4), calls=%async_computation | async-start | bytes 32768 | tf_op jit(solution)/shard_map/slice | solution.py:78
  138.2 4.1 %slice-start.1 = ((f32[1,1,4,128,32]{3,4,2,1,0:T(8,128)}), f32[1,1,1,128,32]{3,4,2,1,0:T(8,128)S(1)}, s32[]{:S(2)}) async-start(f32[1,1,4,128,32]{3,4,2,1,0:T(8,128)} %copy-done.5), calls=%async_computation.1 | async-start | bytes 32768 | tf_op jit(solution)/shard_map/slice | solution.py:78
